TPU v7x, 32 devices: a whole 2x2x4 slice. The times are simulated.
32 devices in a mesh: gx: 4 (over y, x), gy: 2 (over core), row: 4 (over z).
Axes of the slice: x: 2, y: 2, z: 4, core: 2. Of those that a mesh axis runs over, the one named last changes fastest.
Arguments:
- occupancy: int32 [32, 512, 1024], P('row', 'gx', 'gy'), may hold values 0 or 1
- random_draws: bfloat16 [4, 32, 512, 1024], P(None, 'row', 'gx', 'gy'), may hold values from 0 to 1
Outputs:
- coverage: float32 [128, 256], P('gx', 'gy')
- projected: float32 [128, 256], P('gx', 'gy')
All inputs are finite; a program needn't handle non-finite values. No bound on the sum of `occupancy` on one device may be relied on, other than what follows from the above.
Results may differ from a plain program's by a relative error of at most 0.0003.
Values may be sent and summed in bfloat16 or wider, within the bound.
No kernel may reach another device: no remote copies, remote signals or barrier semaphores. Data moves between devices by JAX's collectives and lax.ppermute only.
A program may use at most 64 MiB of HBM per device.

v0:
```python
import jax
import jax.numpy as jnp
from jax import lax
from jax.sharding import PartitionSpec as P

SWEEPS = 4
BLOCK = 4
LEAP = 8
ADSORB = 0.6
DESORB = 0.6
HOPPING = 0.3
COUPLING = 0.5


def padded_2(block, sides, width):
    for axis, dim in sides:
        count = lax.axis_size(axis)
        forward = [(i, i + 1) for i in range(count - 1)]
        forward.append((count - 1, 0))
        backward = [(target, source) for source, target in forward]
        low = lax.ppermute(
            lax.slice_in_dim(block, block.shape[dim] - width, None, axis=dim), axis, forward
        )
        high = lax.ppermute(lax.slice_in_dim(block, 0, width, axis=dim), axis, backward)
        block = jnp.concatenate([low, block, high], axis=dim)
    return block


def sublattice_update(padded, jitter, colour):
    centre = padded[..., 1:-1, 1:-1]
    beside = (
        padded[..., 2:, 1:-1]
        + padded[..., :-2, 1:-1]
        + padded[..., 1:-1, 2:]
        + padded[..., 1:-1, :-2]
    )
    updated = (
        centre
        + ADSORB * jitter * (1.0 - centre)
        - DESORB * (1.0 - jitter) * jnp.exp(-COUPLING * beside) * centre
        + HOPPING * (0.25 * beside - centre)
    )
    row_index = lax.broadcasted_iota(jnp.int32, centre.shape[-2:], 0)
    col_index = lax.broadcasted_iota(jnp.int32, centre.shape[-2:], 1)
    chosen = (row_index + col_index + colour) % 2 == 0
    return jnp.where(chosen[None], updated, centre)


def block_sums(field):
    height, width = (field.shape[-2], field.shape[-1])
    shaped = field.reshape(field.shape[:-2] + (height // BLOCK, BLOCK, width // BLOCK, BLOCK))
    return jnp.sum(shaped, axis=(-3, -1))


def per_device(occupancy, random_draws):
    occupied = occupancy.astype(jnp.float32)
    earlier = occupied
    even_draws = padded_2(random_draws[0::2], (("gx", 2), ("gy", 3)), 1)
    for pair_index in range(SWEEPS // 2):
        if 2 * pair_index == SWEEPS - 2:
            earlier = occupied
        widened = padded_2(occupied, (("gx", 1), ("gy", 2)), 2)
        middle = sublattice_update(widened, even_draws[pair_index].astype(jnp.float32), 0)
        occupied = sublattice_update(
            middle, random_draws[2 * pair_index + 1].astype(jnp.float32), 1
        )
    snapshots = jnp.stack([jnp.sum(earlier, axis=0), jnp.sum(occupied, axis=0)])
    coarse_sums = lax.psum(block_sums(snapshots), "row")
    divisor = jnp.float32(occupancy.shape[0] * lax.axis_size("row") * BLOCK * BLOCK)
    averages = coarse_sums / divisor
    coverage = averages[1]
    projected = coverage + LEAP / 2.0 * (coverage - averages[0])
    return (coverage, projected)


def solution(mesh):
    in_specs = (P("row", "gx", "gy"), P(None, "row", "gx", "gy"))
    out_specs = (P("gx", "gy"), P("gx", "gy"))
    return jax.shard_map(
        per_device, mesh=mesh, in_specs=in_specs, out_specs=out_specs, check_vma=False
    )
```

profile of v0, /device:TPU:0, one launch (start us, length us, event | category | flops | bytes accessed | tf_op | source)
XLA Modules:
  0.0 108.9 jit_solution(14045809891136270607)
XLA Ops:
  0.6 3.0 %copy_convert_fusion = f32[8,128,512]{2,0,1:T(8,128)S(1)} fusion(s32[8,128,512]{2,1,0:T(8,128)} %param.2), kind=kLoop, calls=%fused_computation.76 | loop fusion | flops 524288 | bytes 4194304 | tf_op jit(solution)/shard_map/convert_element_type | solution.py:56
  3.6 3.0 %collective-permute-start = (f32[8,2,512]{2,0,1:T(8,128)S(1)}, f32[8,2,512]{2,0,1:T(8,128)S(1)}, u32[]{:S(2)}, u32[]{:S(2)}) collective-permute-start(f32[8,2,512]{2,0,1:T(8,128)S(1)} %get-tuple-element.18), channel_id=1, source_target_pairs={{0,8},{8,16},{16,24},{24,0},{1,9},{9,17},{17,25},{25,1},{2,10},{10... | collective-permute-start | bytes 98312 | tf_op jit(solution)/shard_map/ppermute | solution.py:21
  6.6 1.0 collective-permute-start.1
  7.7 0.2 slice.126
  7.9 1.1 collective-permute-start.4
  9.0 1.9 %collective-permute-start.5 = (bf16[2,8,1,512]{3,1,2,0:T(8,128)(2,1)S(1)}, bf16[2,8,1,512]{3,1,2,0:T(8,128)(2,1)S(1)}, u32[]{:S(2)}, u32[]{:S(2)}) collective-permute-start(bf16[2,8,1,512]{3,1,2,0:T(8,128)(2,1)S(1)} %copy.54), channel_id=1, source_target_pairs={{8,0},{16,8},{24,16},{0,24},{9,1},{17,9},{25,17},{1,25},{10,2},{18... | collective-permute-start | bytes 49160 | tf_op jit(solution)/shard_map/ppermute | solution.py:24
  10.9 1.5 %fusion.57 = (bf16[1,8,128,512]{3,2,1,0:T(8,128)(2,1)}, bf16[1,8,128,512]{3,2,1,0:T(8,128)(2,1)}) fusion(bf16[4,8,128,512]{3,2,1,0:T(8,128)(2,1)S(1)} %copy-done.3), kind=kLoop, calls=%fused_computation.107 | loop fusion | bytes 4194304 | tf_op jit(solution)/shard_map/slice | solution.py:65
  12.5 0.1 collective-permute-done.4
  12.6 1.2 %constant_dynamic-update-slice_fusion.1 = bf16[2,8,130,512]{3,1,2,0:T(8,128)(2,1)S(1)} fusion(bf16[2,8,130,512]{3,1,2,0:T(8,128)(2,1)S(1)} %constant_dynamic-update-slice_fusion.2, bf16[2,8,128,512]{3,2,1,0:T(8,128)(2,1)S(1)} %slice.126), kind=kLoop, calls=%fused_computation.104 | loop fusion | bytes 4194304
  13.8 1.3 %copy-done.2 = bf16[2,8,130,512]{3,1,2,0:T(8,128)(2,1)} copy-done((bf16[2,8,130,512]{3,1,2,0:T(8,128)(2,1)}, bf16[2,8,130,512]{3,1,2,0:T(8,128)(2,1)S(1)}, u32[]{:S(2)}) %copy-start.2) | copy-done | bytes 2129944
  15.1 0.3 fusion.58
  15.4 0.4 copy.16
  15.9 0.4 copy.17
  16.3 0.5 collective-permute-start.7
  16.9 0.7 fusion.51
  17.6 1.3 %copy.18 = bf16[2,8,130,1]{3,1,2,0:T(8,128)(2,1)} copy(bf16[2,8,130,1]{2,1,3,0:T(8,128)(2,1)S(1)} %collective-permute-done.6) | data formatting | bytes 8320 | tf_op jit(solution)/shard_map/ppermute | solution.py:21
  18.9 1.3 %copy.19 = bf16[2,8,130,1]{3,1,2,0:T(8,128)(2,1)} copy(bf16[2,8,130,1]{2,1,3,0:T(8,128)(2,1)S(1)} %collective-permute-done.7) | data formatting | bytes 8320 | tf_op jit(solution)/shard_map/ppermute | solution.py:24
  20.2 0.2 pad_maximum_fusion.18
  20.4 0.3 copy.11
  20.8 0.3 copy.12
  21.1 0.5 collective-permute-start.3
  21.6 5.0 %pad_maximum_fusion.14 = bf16[2,8,130,514]{3,1,2,0:T(8,128)(2,1)} fusion(bf16[2,8,130,1]{3,1,2,0:T(8,128)(2,1)} %copy.19, bf16[2,8,130,512]{3,1,2,0:T(8,128)(2,1)} %copy-done.2, bf16[2,8,130,1]{3,1,2,0:T(8,128)(2,1)} %copy.18), kind=kLoop, calls=%fused_computation.44 | loop fusion | flops 6414720 | bytes 4276480 | tf_op jit(solution)/shard_map/concatenate | solution.py:25
  26.7 0.4 copy.13
  27.1 0.4 copy.14
  27.5 0.9 pad_maximum_fusion
  28.4 0.8 copy-done
  29.2 4.2 %fusion.5 = f32[8,130,514]{2,0,1:T(8,128)S(1)} fusion(f32[8,2,512]{2,0,1:T(8,128)S(1)} %collective-permute-done.1, f32[8,128,512]{2,0,1:T(8,128)S(1)} %copy_convert_fusion, f32[8,2,512]{2,0,1:T(8,128)S(1)} %collective-permute-done, f32[8,132,2]{2,0,1:T(8,128)S(1)} %copy.13, f32[8,132,2]{2,0,1:T(8,128)S(1)} %copy.14, f32[8,132,516]{2,0,1:T(8,128)S(1)} %pad_maximum_fusion, ...), kind=kLoop, calls=%fused_computation.11 | loop fusion | flops 13364000 | bytes 11868484 | tf_op jit(solution)/shard_map/jit(_where)/select_n | solution.py:46
  33.5 4.6 %fusion.55 = (f32[128,512]{1,0:T(8,128)S(1)}, f32[8,128,512]{2,0,1:T(8,128)S(1)}) fusion(f32[8,130,514]{2,0,1:T(8,128)S(1)} %fusion.5, bf16[1,8,128,512]{3,2,1,0:T(8,128)(2,1)S(1)} %copy-done.5, pred[128,512]{1,0:T(8,128)(4,1)S(1)} %copy-done.6), kind=kLoop, calls=%fused_computation.106 | loop fusion | flops 10420224 | bytes 13959168 | tf_op jit(solution)/shard_map/reduce_sum | solution.py:67
  38.1 2.3 %collective-permute-start.8 = (f32[8,2,512]{2,0,1:T(8,128)S(1)}, f32[8,2,512]{2,0,1:T(8,128)S(1)}, u32[]{:S(2)}, u32[]{:S(2)}) collective-permute-start(f32[8,2,512]{2,0,1:T(8,128)S(1)} %get-tuple-element.14), channel_id=1, source_target_pairs={{0,8},{8,16},{16,24},{24,0},{1,9},{9,17},{17,25},{25,1},{2,10},{10... | collective-permute-start | bytes 98312 | tf_op jit(solution)/shard_map/ppermute | solution.py:21
  40.3 0.7 collective-permute-start.9
  41.1 2.0 %collective-permute-done.8 = f32[8,2,512]{2,0,1:T(8,128)S(1)} collective-permute-done((f32[8,2,512]{2,0,1:T(8,128)S(1)}, f32[8,2,512]{2,0,1:T(8,128)S(1)}, u32[]{:S(2)}, u32[]{:S(2)}) %collective-permute-start.8) | collective-permute-done | bytes 32800 | tf_op jit(solution)/shard_map/ppermute | solution.py:21
  43.1 1.2 %collective-permute-done.9 = f32[8,2,512]{2,0,1:T(8,128)S(1)} collective-permute-done((f32[8,2,512]{2,0,1:T(8,128)S(1)}, f32[8,2,512]{2,0,1:T(8,128)S(1)}, u32[]{:S(2)}, u32[]{:S(2)}) %collective-permute-start.9) | collective-permute-done | bytes 32800 | tf_op jit(solution)/shard_map/ppermute | solution.py:24
  44.3 0.2 pad_maximum_fusion.15
  44.5 0.4 copy-done.10
  44.9 0.3 copy.25
  45.3 0.3 copy.26
  45.6 0.5 collective-permute-start.11
  46.2 10.0 %reshape.78 = f32[1,32,4,128,4]{4,3,2,1,0:T(8,128)} reshape(f32[128,512]{1,0:T(8,128)S(1)} %get-tuple-element.4) | data formatting | bytes 524288 | tf_op jit(solution)/shard_map/stack | solution.py:67
  56.2 5.2 %copy.34 = f32[1,32,4,128,4]{3,1,4,2,0:T(8,128)S(1)} copy(f32[1,32,4,128,4]{4,3,2,1,0:T(8,128)} %reshape.78) | data formatting | bytes 524288 | tf_op jit(solution)/shard_map/stack | solution.py:67
  61.5 0.4 copy.27
  61.9 1.1 %copy.28 = f32[8,132,2]{2,0,1:T(8,128)S(1)} copy(f32[8,132,2]{1,0,2:T(8,128)} %collective-permute-done.11) | data formatting | bytes 16896 | tf_op jit(solution)/shard_map/ppermute | solution.py:24
  63.0 1.8 %pad_maximum_fusion.1 = f32[8,132,516]{2,0,1:T(8,128)S(1)} fusion(f32[8,132,2]{2,0,1:T(8,128)S(1)} %copy.28, f32[8,2,512]{2,0,1:T(8,128)} %copy-done.10, f32[8,128,512]{2,0,1:T(8,128)S(1)} %get-tuple-element.5, f32[8,2,512]{2,0,1:T(8,128)} %copy-done.8, f32[8,132,2]{2,0,1:T(8,128)S(1)} %copy.27), kind=kLoop, calls=%fused_computation.5 | loop fusion | flops 2179584 | bytes 4359168 | tf_op jit(solution)/shard_map/concatenate | solution.py:25
  64.9 4.2 %fusion.15 = f32[8,130,514]{2,0,1:T(8,128)S(1)} fusion(f32[8,2,512]{2,0,1:T(8,128)S(1)} %copy-done.11, f32[8,128,512]{2,0,1:T(8,128)S(1)} %get-tuple-element.5, f32[8,2,512]{2,0,1:T(8,128)S(1)} %copy-done.9, f32[8,132,2]{2,0,1:T(8,128)S(1)} %copy.27, f32[8,132,2]{2,0,1:T(8,128)S(1)} %copy.28, f32[8,132,516]{2,0,1:T(8,128)S(1)} %pad_maximum_fusion.1, ...), kind=kLoop, calls=%fused_computation.21 | loop fusion | flops 13364000 | bytes 11868484 | tf_op jit(solution)/shard_map/jit(_where)/select_n | solution.py:46
  69.2 4.5 %fusion.40 = f32[128,512]{1,0:T(8,128)S(1)} fusion(f32[8,130,514]{2,0,1:T(8,128)S(1)} %fusion.15, bf16[1,8,128,512]{3,2,1,0:T(8,128)(2,1)S(1)} %copy-done.4, pred[128,512]{1,0:T(8,128)(4,1)S(1)} %copy-done.7), kind=kLoop, calls=%fused_computation.65 | loop fusion | flops 10420224 | bytes 11862016 | tf_op jit(solution)/shard_map/reduce_sum | solution.py:67
  73.7 10.0 %reshape.79 = f32[1,32,4,128,4]{4,3,2,1,0:T(8,128)} reshape(f32[128,512]{1,0:T(8,128)S(1)} %fusion.40) | data formatting | bytes 524288 | tf_op jit(solution)/shard_map/stack | solution.py:67
  83.7 5.2 %copy.35 = f32[1,32,4,128,4]{3,1,4,2,0:T(8,128)S(1)} copy(f32[1,32,4,128,4]{4,3,2,1,0:T(8,128)} %reshape.79) | data formatting | bytes 524288 | tf_op jit(solution)/shard_map/stack | solution.py:67
  89.0 19.3 %psum.7 = f32[2,32,128]{2,1,0:T(8,128)S(1)} all-reduce(f32[2,32,128]{2,1,0:T(8,128)S(1)} %maximum_reduce_fusion), channel_id=1, replica_groups=mesh['gx'=4,'gy'=2,'row'=4] {'row'}, use_global_device_ids=true, to_apply=%region_3.4 | all-reduce | flops 8192 | bytes 65536 | tf_op jit(solution)/shard_map/psum | solution.py:68
  108.3 0.6 fusion.54
  (43 shorter events, 0.4 us)
Async XLA Ops:
  0.6 7.0 %copy-start.3 = (bf16[4,8,128,512]{3,2,1,0:T(8,128)(2,1)S(1)}, bf16[4,8,128,512]{3,2,1,0:T(8,128)(2,1)}, u32[]{:S(2)}) copy-start(bf16[4,8,128,512]{3,2,1,0:T(8,128)(2,1)} %param.3) | copy-start | bytes 12582916
  3.6 16.5 %collective-permute-start = (f32[8,2,512]{2,0,1:T(8,128)S(1)}, f32[8,2,512]{2,0,1:T(8,128)S(1)}, u32[]{:S(2)}, u32[]{:S(2)}) collective-permute-start(f32[8,2,512]{2,0,1:T(8,128)S(1)} %get-tuple-element.18), channel_id=1, source_target_pairs={{0,8},{8,16},{16,24},{24,0},{1,9},{9,17},{17,25},{25,1},{2,10},{10... | collective-permute-start | bytes 98312 | tf_op jit(solution)/shard_map/ppermute | solution.py:21
  6.6 13.5 %collective-permute-start.1 = (f32[8,2,512]{2,0,1:T(8,128)S(1)}, f32[8,2,512]{2,0,1:T(8,128)S(1)}, u32[]{:S(2)}, u32[]{:S(2)}) collective-permute-start(f32[8,2,512]{2,0,1:T(8,128)S(1)} %get-tuple-element.19), channel_id=1, source_target_pairs={{8,0},{16,8},{24,16},{0,24},{9,1},{17,9},{25,17},{1,25},{10,2},{18... | collective-permute-start | bytes 98312 | tf_op jit(solution)/shard_map/ppermute | solution.py:24
  7.9 4.7 %collective-permute-start.4 = (bf16[2,8,1,512]{3,1,2,0:T(8,128)(2,1)S(1)}, bf16[2,8,1,512]{3,1,2,0:T(8,128)(2,1)S(1)}, u32[]{:S(2)}, u32[]{:S(2)}) collective-permute-start(bf16[2,8,1,512]{3,1,2,0:T(8,128)(2,1)S(1)} %copy.53), channel_id=1, source_target_pairs={{0,8},{8,16},{16,24},{24,0},{1,9},{9,17},{17,25},{25,1},{2,10},{10... | collective-permute-start | bytes 49160 | tf_op jit(solution)/shard_map/ppermute | solution.py:21
  9.0 4.8 %collective-permute-start.5 = (bf16[2,8,1,512]{3,1,2,0:T(8,128)(2,1)S(1)}, bf16[2,8,1,512]{3,1,2,0:T(8,128)(2,1)S(1)}, u32[]{:S(2)}, u32[]{:S(2)}) collective-permute-start(bf16[2,8,1,512]{3,1,2,0:T(8,128)(2,1)S(1)} %copy.54), channel_id=1, source_target_pairs={{8,0},{16,8},{24,16},{0,24},{9,1},{17,9},{25,17},{1,25},{10,2},{18... | collective-permute-start | bytes 49160 | tf_op jit(solution)/shard_map/ppermute | solution.py:24
  13.8 1.3 %copy-start.2 = (bf16[2,8,130,512]{3,1,2,0:T(8,128)(2,1)}, bf16[2,8,130,512]{3,1,2,0:T(8,128)(2,1)S(1)}, u32[]{:S(2)}) copy-start(bf16[2,8,130,512]{3,1,2,0:T(8,128)(2,1)S(1)} %constant_dynamic-update-slice_fusion) | copy-start | bytes 6389764
  15.8 1.8 %collective-permute-start.6 = (bf16[2,8,130,1]{2,1,3,0:T(8,128)(2,1)S(1)}, bf16[2,8,130,1]{2,1,3,0:T(8,128)(2,1)S(1)}, u32[]{:S(2)}, u32[]{:S(2)}) collective-permute-start(bf16[2,8,130,1]{2,1,3,0:T(8,128)(2,1)S(1)} %copy.16), channel_id=1, source_target_pairs={{0,4},{4,0},{1,5},{5,1},{2,6},{6,2},{3,7},{7,3},{8,12},{12,8},{9,1... | collective-permute-start | bytes 12488 | tf_op jit(solution)/shard_map/ppermute | solution.py:21
  16.3 2.5 %collective-permute-start.7 = (bf16[2,8,130,1]{2,1,3,0:T(8,128)(2,1)S(1)}, bf16[2,8,130,1]{2,1,3,0:T(8,128)(2,1)S(1)}, u32[]{:S(2)}, u32[]{:S(2)}) collective-permute-start(bf16[2,8,130,1]{2,1,3,0:T(8,128)(2,1)S(1)} %copy.17), channel_id=1, source_target_pairs={{4,0},{0,4},{5,1},{1,5},{6,2},{2,6},{7,3},{3,7},{12,8},{8,12},{13,... | collective-permute-start | bytes 12488 | tf_op jit(solution)/shard_map/ppermute | solution.py:24
  20.7 6.0 %collective-permute-start.2 = (f32[8,132,2]{1,0,2:T(8,128)S(1)}, f32[8,132,2]{1,0,2:T(8,128)S(1)}, u32[]{:S(2)}, u32[]{:S(2)}) collective-permute-start(f32[8,132,2]{1,0,2:T(8,128)S(1)} %copy.11), channel_id=1, source_target_pairs={{0,4},{4,0},{1,5},{5,1},{2,6},{6,2},{3,7},{7,3},{8,12},{12,8},{9,1... | collective-permute-start | bytes 25352 | tf_op jit(solution)/shard_map/ppermute | solution.py:21
  21.1 6.0 %collective-permute-start.3 = (f32[8,132,2]{1,0,2:T(8,128)S(1)}, f32[8,132,2]{1,0,2:T(8,128)S(1)}, u32[]{:S(2)}, u32[]{:S(2)}) collective-permute-start(f32[8,132,2]{1,0,2:T(8,128)S(1)} %copy.12), channel_id=1, source_target_pairs={{4,0},{0,4},{5,1},{1,5},{6,2},{2,6},{7,3},{3,7},{12,8},{8,12},{13,... | collective-permute-start | bytes 25352 | tf_op jit(solution)/shard_map/ppermute | solution.py:24
  27.5 1.8 %copy-start = (bf16[2,8,130,514]{3,1,2,0:T(8,128)(2,1)S(1)}, bf16[2,8,130,514]{3,1,2,0:T(8,128)(2,1)}, u32[]{:S(2)}) copy-start(bf16[2,8,130,514]{3,1,2,0:T(8,128)(2,1)} %pad_maximum_fusion.14) | copy-start | bytes 6414724
  29.2 4.2 %copy-start.5 = (bf16[1,8,128,512]{3,2,1,0:T(8,128)(2,1)S(1)}, bf16[1,8,128,512]{3,2,1,0:T(8,128)(2,1)}, u32[]{:S(2)}) copy-start(bf16[1,8,128,512]{3,2,1,0:T(8,128)(2,1)} %get-tuple-element.7) | copy-start | bytes 3145732
  29.2 4.2 %copy-start.6 = (pred[128,512]{1,0:T(8,128)(4,1)S(1)}, pred[128,512]{1,0:T(8,128)(4,1)}, u32[]{:S(2)}) copy-start(pred[128,512]{1,0:T(8,128)(4,1)} %fusion.51) | copy-start | bytes 196612
  38.1 5.0 %collective-permute-start.8 = (f32[8,2,512]{2,0,1:T(8,128)S(1)}, f32[8,2,512]{2,0,1:T(8,128)S(1)}, u32[]{:S(2)}, u32[]{:S(2)}) collective-permute-start(f32[8,2,512]{2,0,1:T(8,128)S(1)} %get-tuple-element.14), channel_id=1, source_target_pairs={{0,8},{8,16},{16,24},{24,0},{1,9},{9,17},{17,25},{25,1},{2,10},{10... | collective-permute-start | bytes 98312 | tf_op jit(solution)/shard_map/ppermute | solution.py:21
  40.3 3.9 %collective-permute-start.9 = (f32[8,2,512]{2,0,1:T(8,128)S(1)}, f32[8,2,512]{2,0,1:T(8,128)S(1)}, u32[]{:S(2)}, u32[]{:S(2)}) collective-permute-start(f32[8,2,512]{2,0,1:T(8,128)S(1)} %get-tuple-element.15), channel_id=1, source_target_pairs={{8,0},{16,8},{24,16},{0,24},{9,1},{17,9},{25,17},{1,25},{10,2},{18... | collective-permute-start | bytes 98312 | tf_op jit(solution)/shard_map/ppermute | solution.py:24
  43.1 1.2 %copy-start.8 = (f32[8,2,512]{2,0,1:T(8,128)}, f32[8,2,512]{2,0,1:T(8,128)S(1)}, u32[]{:S(2)}) copy-start(f32[8,2,512]{2,0,1:T(8,128)S(1)} %collective-permute-done.8) | copy-start | bytes 98308
  44.3 0.6 copy-start.10
  45.2 16.2 %collective-permute-start.10 = (f32[8,132,2]{1,0,2:T(8,128)S(1)}, f32[8,132,2]{1,0,2:T(8,128)S(1)}, u32[]{:S(2)}, u32[]{:S(2)}) collective-permute-start(f32[8,132,2]{1,0,2:T(8,128)S(1)} %copy.25), channel_id=1, source_target_pairs={{0,4},{4,0},{1,5},{5,1},{2,6},{6,2},{3,7},{7,3},{8,12},{12,8},{9,1... | collective-permute-start | bytes 25352 | tf_op jit(solution)/shard_map/ppermute | solution.py:21
  45.6 16.2 %collective-permute-start.11 = (f32[8,132,2]{1,0,2:T(8,128)S(1)}, f32[8,132,2]{1,0,2:T(8,128)}, u32[]{:S(2)}, u32[]{:S(2)}) collective-permute-start(f32[8,132,2]{1,0,2:T(8,128)S(1)} %copy.26), channel_id=1, source_target_pairs={{4,0},{0,4},{5,1},{1,5},{6,2},{2,6},{7,3},{3,7},{12,8},{8,12},{13,... | collective-permute-start | bytes 25352 | tf_op jit(solution)/shard_map/ppermute | solution.py:24
  63.0 1.9 %copy-start.1 = (bf16[2,8,130,514]{3,1,2,0:T(8,128)(2,1)S(1)}, bf16[2,8,130,514]{3,1,2,0:T(8,128)(2,1)}, u32[]{:S(2)}) copy-start(bf16[2,8,130,514]{3,1,2,0:T(8,128)(2,1)} %pad_maximum_fusion.14) | copy-start | bytes 6414724
  63.0 1.9 %copy-start.9 = (f32[8,2,512]{2,0,1:T(8,128)S(1)}, f32[8,2,512]{2,0,1:T(8,128)}, u32[]{:S(2)}) copy-start(f32[8,2,512]{2,0,1:T(8,128)} %copy-done.8) | copy-start | bytes 98308
  63.0 1.9 %copy-start.11 = (f32[8,2,512]{2,0,1:T(8,128)S(1)}, f32[8,2,512]{2,0,1:T(8,128)}, u32[]{:S(2)}) copy-start(f32[8,2,512]{2,0,1:T(8,128)} %copy-done.10) | copy-start | bytes 98308
  64.9 4.3 %copy-start.4 = (bf16[1,8,128,512]{3,2,1,0:T(8,128)(2,1)S(1)}, bf16[1,8,128,512]{3,2,1,0:T(8,128)(2,1)}, u32[]{:S(2)}) copy-start(bf16[1,8,128,512]{3,2,1,0:T(8,128)(2,1)} %get-tuple-element.6) | copy-start | bytes 3145732
  64.9 4.3 %copy-start.7 = (pred[128,512]{1,0:T(8,128)(4,1)S(1)}, pred[128,512]{1,0:T(8,128)(4,1)}, u32[]{:S(2)}) copy-start(pred[128,512]{1,0:T(8,128)(4,1)} %fusion.51) | copy-start | bytes 196612
where the time goes:
time: 109 us
  local copies, waits for them, and re-layouts  43.4 us (40%)
  other arithmetic  30.1 us (28%)
  blocking collectives  19.3 us (18%)
  starting transfers between devices  11.8 us (11%)
  waiting for transfers between devices  3.33 us (3%)
    another operation x4, local copies, waits for them, and re-layouts, per_device(): snapshots = jnp.stack([jnp.sum(earlier, axis=0), jnp.sum(occupied, axis=0)])  30.5 us
    psum x1, blocking collectives, per_device(): coarse_sums = lax.psum(block_sums(snapshots), 'row')  19.3 us
    reduce_sum x2, other arithmetic, per_device(): snapshots = jnp.stack([jnp.sum(earlier, axis=0), jnp.sum(occupied, axis=0)])  9.11 us
    select_n x2, other arithmetic, sublattice_update(): return jnp.where(chosen[None], updated, centre)  8.46 us
    concatenate x5, other arithmetic, padded_2(): block = jnp.concatenate([low, block, high], axis=dim)  8.14 us
    ppermute x6, starting transfers between devices, padded_2(): lax.ppermute(lax.slice_in_dim(block, block.shape[dim] - width, None, axis...  6.51 us
    ppermute x6, starting transfers between devices, padded_2(): lax.ppermute(lax.slice_in_dim(block, 0, width, axis=dim), axis, backward)  5.3 us
    unnamed x28, local copies, waits for them, and re-layouts  3.81 us
  transfers between devices with their start and end apart: 12, of which 3 were waited for; matrix products, arithmetic and copies ran while one was open for 27% of the time, Pallas kernels for 0%

commit v1 on v0

--- a/solution.py
+++ b/solution.py
@@ -65,7 +65,7 @@
             middle, random_draws[2 * pair_index + 1].astype(jnp.float32), 1
         )
     snapshots = jnp.stack([jnp.sum(earlier, axis=0), jnp.sum(occupied, axis=0)])
-    coarse_sums = lax.psum(block_sums(snapshots), "row")
+    coarse_sums = jnp.sum(lax.all_gather(block_sums(snapshots), "row"), axis=0)
     divisor = jnp.float32(occupancy.shape[0] * lax.axis_size("row") * BLOCK * BLOCK)
     averages = coarse_sums / divisor
     coverage = averages[1]

time: 109 us -> 104 us (0.954)
  blocking collectives: 19.3 us -> 13.6 us
    psum x1 -> x0, blocking collectives: 19.3 us -> none  [per_device(): coarse_sums = lax.psum(block_sums(snapshots), 'row')]
    all_gather x0 -> x1, blocking collectives: none -> 13.6 us  [per_device(): coarse_sums = jnp.sum(lax.all_gather(block_sums(snapshots), 'row'), axis=0)]
  transfers between devices with their start and end apart: 12 -> 12, of which waited for: 3 -> 3; matrix products, arithmetic and copies ran while one was open for 27% -> 28% of each run, Pallas kernels for 0% -> 0%
where the time goes in v1:
time: 104 us; the launch traced here: 103 us
  local copies, waits for them, and re-layouts  43.4 us (42%)
  other arithmetic  30.2 us (29%)
  blocking collectives  13.6 us (13%)
  starting transfers between devices  11.8 us (11%)
  waiting for transfers between devices  3.33 us (3%)
    another operation x4, local copies, waits for them, and re-layouts, per_device(): snapshots = jnp.stack([jnp.sum(earlier, axis=0), jnp.sum(occupied, axis=0)])  30.5 us
    all_gather x1, blocking collectives, per_device(): coarse_sums = jnp.sum(lax.all_gather(block_sums(snapshots), 'row'), axis=0)  13.6 us
    reduce_sum x2, other arithmetic, per_device(): snapshots = jnp.stack([jnp.sum(earlier, axis=0), jnp.sum(occupied, axis=0)])  9.11 us
    select_n x2, other arithmetic, sublattice_update(): return jnp.where(chosen[None], updated, centre)  8.46 us
    concatenate x5, other arithmetic, padded_2(): block = jnp.concatenate([low, block, high], axis=dim)  8.14 us
    ppermute x6, starting transfers between devices, padded_2(): lax.ppermute(lax.slice_in_dim(block, block.shape[dim] - width, None, axis...  6.51 us
    ppermute x6, starting transfers between devices, padded_2(): lax.ppermute(lax.slice_in_dim(block, 0, width, axis=dim), axis, backward)  5.3 us
    unnamed x28, local copies, waits for them, and re-layouts  3.81 us
  transfers between devices with their start and end apart: 12, of which 3 were waited for; matrix products, arithmetic and copies ran while one was open for 28% of the time, Pallas kernels for 0%

profile of v1, /device:TPU:0, one launch (start us, length us, event | category | flops | bytes accessed | tf_op | source)
XLA Modules:
  0.0 103.3 jit_solution(14946772880536103160)
XLA Ops:
  0.6 3.0 %copy_convert_fusion = f32[8,128,512]{2,0,1:T(8,128)S(1)} fusion(s32[8,128,512]{2,1,0:T(8,128)} %param.2), kind=kLoop, calls=%fused_computation.76 | loop fusion | flops 524288 | bytes 4194304 | tf_op jit(solution)/shard_map/convert_element_type | solution.py:56
  3.6 3.0 %collective-permute-start = (f32[8,2,512]{2,0,1:T(8,128)S(1)}, f32[8,2,512]{2,0,1:T(8,128)S(1)}, u32[]{:S(2)}, u32[]{:S(2)}) collective-permute-start(f32[8,2,512]{2,0,1:T(8,128)S(1)} %get-tuple-element.18), channel_id=1, source_target_pairs={{0,8},{8,16},{16,24},{24,0},{1,9},{9,17},{17,25},{25,1},{2,10},{10... | collective-permute-start | bytes 98312 | tf_op jit(solution)/shard_map/ppermute | solution.py:21
  6.6 1.0 collective-permute-start.1
  7.7 0.2 slice.126
  7.9 1.1 %collective-permute-start.4 = (bf16[2,8,1,512]{3,1,2,0:T(8,128)(2,1)S(1)}, bf16[2,8,1,512]{3,1,2,0:T(8,128)(2,1)S(1)}, u32[]{:S(2)}, u32[]{:S(2)}) collective-permute-start(bf16[2,8,1,512]{3,1,2,0:T(8,128)(2,1)S(1)} %copy.53), channel_id=1, source_target_pairs={{0,8},{8,16},{16,24},{24,0},{1,9},{9,17},{17,25},{25,1},{2,10},{10... | collective-permute-start | bytes 49160 | tf_op jit(solution)/shard_map/ppermute | solution.py:21
  9.0 1.9 %collective-permute-start.5 = (bf16[2,8,1,512]{3,1,2,0:T(8,128)(2,1)S(1)}, bf16[2,8,1,512]{3,1,2,0:T(8,128)(2,1)S(1)}, u32[]{:S(2)}, u32[]{:S(2)}) collective-permute-start(bf16[2,8,1,512]{3,1,2,0:T(8,128)(2,1)S(1)} %copy.54), channel_id=1, source_target_pairs={{8,0},{16,8},{24,16},{0,24},{9,1},{17,9},{25,17},{1,25},{10,2},{18... | collective-permute-start | bytes 49160 | tf_op jit(solution)/shard_map/ppermute | solution.py:24
  10.9 1.5 %fusion.57 = (bf16[1,8,128,512]{3,2,1,0:T(8,128)(2,1)}, bf16[1,8,128,512]{3,2,1,0:T(8,128)(2,1)}) fusion(bf16[4,8,128,512]{3,2,1,0:T(8,128)(2,1)S(1)} %copy-done.3), kind=kLoop, calls=%fused_computation.107 | loop fusion | bytes 4194304 | tf_op jit(solution)/shard_map/slice | solution.py:65
  12.5 0.1 collective-permute-done.4
  12.6 1.2 %constant_dynamic-update-slice_fusion.1 = bf16[2,8,130,512]{3,1,2,0:T(8,128)(2,1)S(1)} fusion(bf16[2,8,130,512]{3,1,2,0:T(8,128)(2,1)S(1)} %constant_dynamic-update-slice_fusion.2, bf16[2,8,128,512]{3,2,1,0:T(8,128)(2,1)S(1)} %slice.126), kind=kLoop, calls=%fused_computation.104 | loop fusion | bytes 4194304
  13.8 1.3 %copy-done.2 = bf16[2,8,130,512]{3,1,2,0:T(8,128)(2,1)} copy-done((bf16[2,8,130,512]{3,1,2,0:T(8,128)(2,1)}, bf16[2,8,130,512]{3,1,2,0:T(8,128)(2,1)S(1)}, u32[]{:S(2)}) %copy-start.2) | copy-done | bytes 2129944
  15.1 0.3 fusion.58
  15.4 0.4 copy.16
  15.9 0.4 copy.17
  16.3 0.5 collective-permute-start.7
  16.9 0.7 fusion.51
  17.6 1.3 %copy.18 = bf16[2,8,130,1]{3,1,2,0:T(8,128)(2,1)} copy(bf16[2,8,130,1]{2,1,3,0:T(8,128)(2,1)S(1)} %collective-permute-done.6) | data formatting | bytes 8320 | tf_op jit(solution)/shard_map/ppermute | solution.py:21
  18.9 1.3 %copy.19 = bf16[2,8,130,1]{3,1,2,0:T(8,128)(2,1)} copy(bf16[2,8,130,1]{2,1,3,0:T(8,128)(2,1)S(1)} %collective-permute-done.7) | data formatting | bytes 8320 | tf_op jit(solution)/shard_map/ppermute | solution.py:24
  20.2 0.2 pad_maximum_fusion.18
  20.4 0.3 copy.11
  20.8 0.3 copy.12
  21.1 0.5 collective-permute-start.3
  21.6 5.0 %pad_maximum_fusion.14 = bf16[2,8,130,514]{3,1,2,0:T(8,128)(2,1)} fusion(bf16[2,8,130,1]{3,1,2,0:T(8,128)(2,1)} %copy.19, bf16[2,8,130,512]{3,1,2,0:T(8,128)(2,1)} %copy-done.2, bf16[2,8,130,1]{3,1,2,0:T(8,128)(2,1)} %copy.18), kind=kLoop, calls=%fused_computation.44 | loop fusion | flops 6414720 | bytes 4276480 | tf_op jit(solution)/shard_map/concatenate | solution.py:25
  26.7 0.4 copy.13
  27.1 0.4 copy.14
  27.5 0.9 pad_maximum_fusion
  28.4 0.8 copy-done
  29.2 4.2 %fusion.5 = f32[8,130,514]{2,0,1:T(8,128)S(1)} fusion(f32[8,2,512]{2,0,1:T(8,128)S(1)} %collective-permute-done.1, f32[8,128,512]{2,0,1:T(8,128)S(1)} %copy_convert_fusion, f32[8,2,512]{2,0,1:T(8,128)S(1)} %collective-permute-done, f32[8,132,2]{2,0,1:T(8,128)S(1)} %copy.13, f32[8,132,2]{2,0,1:T(8,128)S(1)} %copy.14, f32[8,132,516]{2,0,1:T(8,128)S(1)} %pad_maximum_fusion, ...), kind=kLoop, calls=%fused_computation.11 | loop fusion | flops 13364000 | bytes 11868484 | tf_op jit(solution)/shard_map/jit(_where)/select_n | solution.py:46
  33.5 4.6 %fusion.55 = (f32[128,512]{1,0:T(8,128)S(1)}, f32[8,128,512]{2,0,1:T(8,128)S(1)}) fusion(f32[8,130,514]{2,0,1:T(8,128)S(1)} %fusion.5, bf16[1,8,128,512]{3,2,1,0:T(8,128)(2,1)S(1)} %copy-done.5, pred[128,512]{1,0:T(8,128)(4,1)S(1)} %copy-done.6), kind=kLoop, calls=%fused_computation.106 | loop fusion | flops 10420224 | bytes 13959168 | tf_op jit(solution)/shard_map/reduce_sum | solution.py:67
  38.1 2.3 %collective-permute-start.8 = (f32[8,2,512]{2,0,1:T(8,128)S(1)}, f32[8,2,512]{2,0,1:T(8,128)S(1)}, u32[]{:S(2)}, u32[]{:S(2)}) collective-permute-start(f32[8,2,512]{2,0,1:T(8,128)S(1)} %get-tuple-element.14), channel_id=1, source_target_pairs={{0,8},{8,16},{16,24},{24,0},{1,9},{9,17},{17,25},{25,1},{2,10},{10... | collective-permute-start | bytes 98312 | tf_op jit(solution)/shard_map/ppermute | solution.py:21
  40.3 0.7 collective-permute-start.9
  41.1 2.0 %collective-permute-done.8 = f32[8,2,512]{2,0,1:T(8,128)S(1)} collective-permute-done((f32[8,2,512]{2,0,1:T(8,128)S(1)}, f32[8,2,512]{2,0,1:T(8,128)S(1)}, u32[]{:S(2)}, u32[]{:S(2)}) %collective-permute-start.8) | collective-permute-done | bytes 32800 | tf_op jit(solution)/shard_map/ppermute | solution.py:21
  43.1 1.2 %collective-permute-done.9 = f32[8,2,512]{2,0,1:T(8,128)S(1)} collective-permute-done((f32[8,2,512]{2,0,1:T(8,128)S(1)}, f32[8,2,512]{2,0,1:T(8,128)S(1)}, u32[]{:S(2)}, u32[]{:S(2)}) %collective-permute-start.9) | collective-permute-done | bytes 32800 | tf_op jit(solution)/shard_map/ppermute | solution.py:24
  44.3 0.2 pad_maximum_fusion.15
  44.5 0.4 copy-done.10
  44.9 0.3 copy.25
  45.3 0.3 copy.26
  45.6 0.5 collective-permute-start.11
  46.2 10.0 %reshape.79 = f32[1,32,4,128,4]{4,3,2,1,0:T(8,128)} reshape(f32[128,512]{1,0:T(8,128)S(1)} %get-tuple-element.4) | data formatting | bytes 524288 | tf_op jit(solution)/shard_map/stack | solution.py:67
  56.2 5.2 %copy.34 = f32[1,32,4,128,4]{3,1,4,2,0:T(8,128)S(1)} copy(f32[1,32,4,128,4]{4,3,2,1,0:T(8,128)} %reshape.79) | data formatting | bytes 524288 | tf_op jit(solution)/shard_map/stack | solution.py:67
  61.5 0.4 copy.27
  61.9 1.1 %copy.28 = f32[8,132,2]{2,0,1:T(8,128)S(1)} copy(f32[8,132,2]{1,0,2:T(8,128)} %collective-permute-done.11) | data formatting | bytes 16896 | tf_op jit(solution)/shard_map/ppermute | solution.py:24
  63.0 1.8 %pad_maximum_fusion.1 = f32[8,132,516]{2,0,1:T(8,128)S(1)} fusion(f32[8,132,2]{2,0,1:T(8,128)S(1)} %copy.28, f32[8,2,512]{2,0,1:T(8,128)} %copy-done.10, f32[8,128,512]{2,0,1:T(8,128)S(1)} %get-tuple-element.5, f32[8,2,512]{2,0,1:T(8,128)} %copy-done.8, f32[8,132,2]{2,0,1:T(8,128)S(1)} %copy.27), kind=kLoop, calls=%fused_computation.5 | loop fusion | flops 2179584 | bytes 4359168 | tf_op jit(solution)/shard_map/concatenate | solution.py:25
  64.9 4.2 %fusion.15 = f32[8,130,514]{2,0,1:T(8,128)S(1)} fusion(f32[8,2,512]{2,0,1:T(8,128)S(1)} %copy-done.11, f32[8,128,512]{2,0,1:T(8,128)S(1)} %get-tuple-element.5, f32[8,2,512]{2,0,1:T(8,128)S(1)} %copy-done.9, f32[8,132,2]{2,0,1:T(8,128)S(1)} %copy.27, f32[8,132,2]{2,0,1:T(8,128)S(1)} %copy.28, f32[8,132,516]{2,0,1:T(8,128)S(1)} %pad_maximum_fusion.1, ...), kind=kLoop, calls=%fused_computation.21 | loop fusion | flops 13364000 | bytes 11868484 | tf_op jit(solution)/shard_map/jit(_where)/select_n | solution.py:46
  69.2 4.5 %fusion.40 = f32[128,512]{1,0:T(8,128)S(1)} fusion(f32[8,130,514]{2,0,1:T(8,128)S(1)} %fusion.15, bf16[1,8,128,512]{3,2,1,0:T(8,128)(2,1)S(1)} %copy-done.4, pred[128,512]{1,0:T(8,128)(4,1)S(1)} %copy-done.7), kind=kLoop, calls=%fused_computation.65 | loop fusion | flops 10420224 | bytes 11862016 | tf_op jit(solution)/shard_map/reduce_sum | solution.py:67
  73.7 10.0 %reshape.80 = f32[1,32,4,128,4]{4,3,2,1,0:T(8,128)} reshape(f32[128,512]{1,0:T(8,128)S(1)} %fusion.40) | data formatting | bytes 524288 | tf_op jit(solution)/shard_map/stack | solution.py:67
  83.7 5.2 %copy.35 = f32[1,32,4,128,4]{3,1,4,2,0:T(8,128)S(1)} copy(f32[1,32,4,128,4]{4,3,2,1,0:T(8,128)} %reshape.80) | data formatting | bytes 524288 | tf_op jit(solution)/shard_map/stack | solution.py:67
  89.0 13.6 %all-gather = f32[8,32,128]{2,1,0:T(8,128)S(1)} all-gather(f32[2,32,128]{2,1,0:T(8,128)S(1)} %maximum_reduce_fusion), channel_id=2, replica_groups=mesh['gx'=4,'gy'=2,'row'=4] {'row'}, dimensions={0}, use_global_device_ids=true | all-gather | bytes 163840 | tf_op jit(solution)/shard_map/all_gather | solution.py:68
  102.6 0.6 fusion.54
  (44 shorter events, 0.5 us)
Async XLA Ops:
  0.6 7.0 %copy-start.3 = (bf16[4,8,128,512]{3,2,1,0:T(8,128)(2,1)S(1)}, bf16[4,8,128,512]{3,2,1,0:T(8,128)(2,1)}, u32[]{:S(2)}) copy-start(bf16[4,8,128,512]{3,2,1,0:T(8,128)(2,1)} %param.3) | copy-start | bytes 12582916
  3.6 16.5 %collective-permute-start = (f32[8,2,512]{2,0,1:T(8,128)S(1)}, f32[8,2,512]{2,0,1:T(8,128)S(1)}, u32[]{:S(2)}, u32[]{:S(2)}) collective-permute-start(f32[8,2,512]{2,0,1:T(8,128)S(1)} %get-tuple-element.18), channel_id=1, source_target_pairs={{0,8},{8,16},{16,24},{24,0},{1,9},{9,17},{17,25},{25,1},{2,10},{10... | collective-permute-start | bytes 98312 | tf_op jit(solution)/shard_map/ppermute | solution.py:21
  6.6 13.5 %collective-permute-start.1 = (f32[8,2,512]{2,0,1:T(8,128)S(1)}, f32[8,2,512]{2,0,1:T(8,128)S(1)}, u32[]{:S(2)}, u32[]{:S(2)}) collective-permute-start(f32[8,2,512]{2,0,1:T(8,128)S(1)} %get-tuple-element.19), channel_id=1, source_target_pairs={{8,0},{16,8},{24,16},{0,24},{9,1},{17,9},{25,17},{1,25},{10,2},{18... | collective-permute-start | bytes 98312 | tf_op jit(solution)/shard_map/ppermute | solution.py:24
  7.9 4.7 %collective-permute-start.4 = (bf16[2,8,1,512]{3,1,2,0:T(8,128)(2,1)S(1)}, bf16[2,8,1,512]{3,1,2,0:T(8,128)(2,1)S(1)}, u32[]{:S(2)}, u32[]{:S(2)}) collective-permute-start(bf16[2,8,1,512]{3,1,2,0:T(8,128)(2,1)S(1)} %copy.53), channel_id=1, source_target_pairs={{0,8},{8,16},{16,24},{24,0},{1,9},{9,17},{17,25},{25,1},{2,10},{10... | collective-permute-start | bytes 49160 | tf_op jit(solution)/shard_map/ppermute | solution.py:21
  9.0 4.8 %collective-permute-start.5 = (bf16[2,8,1,512]{3,1,2,0:T(8,128)(2,1)S(1)}, bf16[2,8,1,512]{3,1,2,0:T(8,128)(2,1)S(1)}, u32[]{:S(2)}, u32[]{:S(2)}) collective-permute-start(bf16[2,8,1,512]{3,1,2,0:T(8,128)(2,1)S(1)} %copy.54), channel_id=1, source_target_pairs={{8,0},{16,8},{24,16},{0,24},{9,1},{17,9},{25,17},{1,25},{10,2},{18... | collective-permute-start | bytes 49160 | tf_op jit(solution)/shard_map/ppermute | solution.py:24
  13.8 1.3 %copy-start.2 = (bf16[2,8,130,512]{3,1,2,0:T(8,128)(2,1)}, bf16[2,8,130,512]{3,1,2,0:T(8,128)(2,1)S(1)}, u32[]{:S(2)}) copy-start(bf16[2,8,130,512]{3,1,2,0:T(8,128)(2,1)S(1)} %constant_dynamic-update-slice_fusion) | copy-start | bytes 6389764
  15.8 1.8 %collective-permute-start.6 = (bf16[2,8,130,1]{2,1,3,0:T(8,128)(2,1)S(1)}, bf16[2,8,130,1]{2,1,3,0:T(8,128)(2,1)S(1)}, u32[]{:S(2)}, u32[]{:S(2)}) collective-permute-start(bf16[2,8,130,1]{2,1,3,0:T(8,128)(2,1)S(1)} %copy.16), channel_id=1, source_target_pairs={{0,4},{4,0},{1,5},{5,1},{2,6},{6,2},{3,7},{7,3},{8,12},{12,8},{9,1... | collective-permute-start | bytes 12488 | tf_op jit(solution)/shard_map/ppermute | solution.py:21
  16.3 2.5 %collective-permute-start.7 = (bf16[2,8,130,1]{2,1,3,0:T(8,128)(2,1)S(1)}, bf16[2,8,130,1]{2,1,3,0:T(8,128)(2,1)S(1)}, u32[]{:S(2)}, u32[]{:S(2)}) collective-permute-start(bf16[2,8,130,1]{2,1,3,0:T(8,128)(2,1)S(1)} %copy.17), channel_id=1, source_target_pairs={{4,0},{0,4},{5,1},{1,5},{6,2},{2,6},{7,3},{3,7},{12,8},{8,12},{13,... | collective-permute-start | bytes 12488 | tf_op jit(solution)/shard_map/ppermute | solution.py:24
  20.7 6.0 %collective-permute-start.2 = (f32[8,132,2]{1,0,2:T(8,128)S(1)}, f32[8,132,2]{1,0,2:T(8,128)S(1)}, u32[]{:S(2)}, u32[]{:S(2)}) collective-permute-start(f32[8,132,2]{1,0,2:T(8,128)S(1)} %copy.11), channel_id=1, source_target_pairs={{0,4},{4,0},{1,5},{5,1},{2,6},{6,2},{3,7},{7,3},{8,12},{12,8},{9,1... | collective-permute-start | bytes 25352 | tf_op jit(solution)/shard_map/ppermute | solution.py:21
  21.1 6.0 %collective-permute-start.3 = (f32[8,132,2]{1,0,2:T(8,128)S(1)}, f32[8,132,2]{1,0,2:T(8,128)S(1)}, u32[]{:S(2)}, u32[]{:S(2)}) collective-permute-start(f32[8,132,2]{1,0,2:T(8,128)S(1)} %copy.12), channel_id=1, source_target_pairs={{4,0},{0,4},{5,1},{1,5},{6,2},{2,6},{7,3},{3,7},{12,8},{8,12},{13,... | collective-permute-start | bytes 25352 | tf_op jit(solution)/shard_map/ppermute | solution.py:24
  27.5 1.8 %copy-start = (bf16[2,8,130,514]{3,1,2,0:T(8,128)(2,1)S(1)}, bf16[2,8,130,514]{3,1,2,0:T(8,128)(2,1)}, u32[]{:S(2)}) copy-start(bf16[2,8,130,514]{3,1,2,0:T(8,128)(2,1)} %pad_maximum_fusion.14) | copy-start | bytes 6414724
  29.2 4.2 %copy-start.5 = (bf16[1,8,128,512]{3,2,1,0:T(8,128)(2,1)S(1)}, bf16[1,8,128,512]{3,2,1,0:T(8,128)(2,1)}, u32[]{:S(2)}) copy-start(bf16[1,8,128,512]{3,2,1,0:T(8,128)(2,1)} %get-tuple-element.7) | copy-start | bytes 3145732
  29.2 4.2 %copy-start.6 = (pred[128,512]{1,0:T(8,128)(4,1)S(1)}, pred[128,512]{1,0:T(8,128)(4,1)}, u32[]{:S(2)}) copy-start(pred[128,512]{1,0:T(8,128)(4,1)} %fusion.51) | copy-start | bytes 196612
  38.1 5.0 %collective-permute-start.8 = (f32[8,2,512]{2,0,1:T(8,128)S(1)}, f32[8,2,512]{2,0,1:T(8,128)S(1)}, u32[]{:S(2)}, u32[]{:S(2)}) collective-permute-start(f32[8,2,512]{2,0,1:T(8,128)S(1)} %get-tuple-element.14), channel_id=1, source_target_pairs={{0,8},{8,16},{16,24},{24,0},{1,9},{9,17},{17,25},{25,1},{2,10},{10... | collective-permute-start | bytes 98312 | tf_op jit(solution)/shard_map/ppermute | solution.py:21
  40.3 3.9 %collective-permute-start.9 = (f32[8,2,512]{2,0,1:T(8,128)S(1)}, f32[8,2,512]{2,0,1:T(8,128)S(1)}, u32[]{:S(2)}, u32[]{:S(2)}) collective-permute-start(f32[8,2,512]{2,0,1:T(8,128)S(1)} %get-tuple-element.15), channel_id=1, source_target_pairs={{8,0},{16,8},{24,16},{0,24},{9,1},{17,9},{25,17},{1,25},{10,2},{18... | collective-permute-start | bytes 98312 | tf_op jit(solution)/shard_map/ppermute | solution.py:24
  43.1 1.2 %copy-start.8 = (f32[8,2,512]{2,0,1:T(8,128)}, f32[8,2,512]{2,0,1:T(8,128)S(1)}, u32[]{:S(2)}) copy-start(f32[8,2,512]{2,0,1:T(8,128)S(1)} %collective-permute-done.8) | copy-start | bytes 98308
  44.3 0.6 copy-start.10
  45.2 16.2 %collective-permute-start.10 = (f32[8,132,2]{1,0,2:T(8,128)S(1)}, f32[8,132,2]{1,0,2:T(8,128)S(1)}, u32[]{:S(2)}, u32[]{:S(2)}) collective-permute-start(f32[8,132,2]{1,0,2:T(8,128)S(1)} %copy.25), channel_id=1, source_target_pairs={{0,4},{4,0},{1,5},{5,1},{2,6},{6,2},{3,7},{7,3},{8,12},{12,8},{9,1... | collective-permute-start | bytes 25352 | tf_op jit(solution)/shard_map/ppermute | solution.py:21
  45.6 16.2 %collective-permute-start.11 = (f32[8,132,2]{1,0,2:T(8,128)S(1)}, f32[8,132,2]{1,0,2:T(8,128)}, u32[]{:S(2)}, u32[]{:S(2)}) collective-permute-start(f32[8,132,2]{1,0,2:T(8,128)S(1)} %copy.26), channel_id=1, source_target_pairs={{4,0},{0,4},{5,1},{1,5},{6,2},{2,6},{7,3},{3,7},{12,8},{8,12},{13,... | collective-permute-start | bytes 25352 | tf_op jit(solution)/shard_map/ppermute | solution.py:24
  63.0 1.9 %copy-start.1 = (bf16[2,8,130,514]{3,1,2,0:T(8,128)(2,1)S(1)}, bf16[2,8,130,514]{3,1,2,0:T(8,128)(2,1)}, u32[]{:S(2)}) copy-start(bf16[2,8,130,514]{3,1,2,0:T(8,128)(2,1)} %pad_maximum_fusion.14) | copy-start | bytes 6414724
  63.0 1.9 %copy-start.9 = (f32[8,2,512]{2,0,1:T(8,128)S(1)}, f32[8,2,512]{2,0,1:T(8,128)}, u32[]{:S(2)}) copy-start(f32[8,2,512]{2,0,1:T(8,128)} %copy-done.8) | copy-start | bytes 98308
  63.0 1.9 %copy-start.11 = (f32[8,2,512]{2,0,1:T(8,128)S(1)}, f32[8,2,512]{2,0,1:T(8,128)}, u32[]{:S(2)}) copy-start(f32[8,2,512]{2,0,1:T(8,128)} %copy-done.10) | copy-start | bytes 98308
  64.9 4.3 %copy-start.4 = (bf16[1,8,128,512]{3,2,1,0:T(8,128)(2,1)S(1)}, bf16[1,8,128,512]{3,2,1,0:T(8,128)(2,1)}, u32[]{:S(2)}) copy-start(bf16[1,8,128,512]{3,2,1,0:T(8,128)(2,1)} %get-tuple-element.6) | copy-start | bytes 3145732
  64.9 4.3 %copy-start.7 = (pred[128,512]{1,0:T(8,128)(4,1)S(1)}, pred[128,512]{1,0:T(8,128)(4,1)}, u32[]{:S(2)}) copy-start(pred[128,512]{1,0:T(8,128)(4,1)} %fusion.51) | copy-start | bytes 196612
